TPU v7x, 128 devices: a whole 4x4x4 slice. The times are simulated.
128 devices in a mesh: seq: 64 (over x, z, y), head: 2 (over core).
Axes of the slice: x: 4, y: 4, z: 4, core: 2. Of those that a mesh axis runs over, the one named last changes fastest.
Arguments:
- queries: bfloat16 [16384, 4096], P('seq', 'head'), may hold values from -210 to 210
- keys: bfloat16 [16384, 1024], P('seq', 'head'), may hold values from -7 to 7
- values: bfloat16 [16384, 1024], P('seq', 'head'), may hold values from -6 to 6
- vertical: int32 [8, 64], P('head'), may hold values from 0 to 255, as said below
- slash: int32 [8, 2], P('head'), may hold values from 1 to 4, as said below
- out_weight: bfloat16 [4096, 4096], P('head'), may hold values from -1 to 1
Outputs:
- mixed: bfloat16 [16384, 4096], P(('seq', 'head'))
Inputs may be any that keep to these rules, and one draw needn't show every extreme that they name: `vertical`: for each key-value head, 64 different key blocks in increasing order; block b lies in slab b // 4; no slab holds more than 2 of one head's blocks, and for every head some slab holds exactly 2. `slash`: for each key-value head, 2 different offsets in increasing order; some head has the offset 256 // 64.
All inputs are finite; a program needn't handle non-finite values.
Results may differ from a plain program's by a relative error of at most 0.01.
Values may be sent and summed in bfloat16 or wider, within the bound.
A program may use at most 128 MiB of HBM per device.

v0:
```python
import math

import jax
import jax.numpy as jnp
from jax import lax
from jax.sharding import PartitionSpec as P

HEAD_DIM = 128
BLK = 64
CAP = 2


NEGATIVE = -1e30


def from_behind(shard, axis, by):
    peers = lax.axis_size(axis)
    pairs = [(i, i + by) for i in range(peers) if 0 <= i + by < peers]
    return lax.ppermute(shard, axis, pairs)


def sent_together(arrays, axis, dim, along):
    both = jnp.concatenate(arrays, axis=along)
    filled, at, gathered = (lax.all_gather(both, axis, axis=dim, tiled=True), 0, [])
    for a in arrays:
        gathered.append(lax.slice_in_dim(filled, at, at + a.shape[along], axis=along))
        at += a.shape[along]
    return tuple(gathered)


def in_blocks(shard, dim, peers):
    before, after = (shard.shape[:dim], shard.shape[dim + 1 :])
    return jnp.moveaxis(shard.reshape(*before, peers, -1, *after), dim, 0)


def summed_on_arrival(shard, axis, dim):
    tiles = in_blocks(shard, dim, lax.axis_size(axis))
    arrived = lax.all_to_all(tiles, axis, split_axis=0, concat_axis=0, tiled=True)
    return arrived.astype(jnp.float32).sum(axis=0)


def spread(blockwise):
    return jnp.repeat(jnp.repeat(blockwise, BLK, axis=1), BLK, axis=2)


def attend(running, query_view, key_part, value_part, allowed):
    top_score, sum_weight, accumulated = running
    scores = jnp.einsum(
        "shgd,khd->hgsk", query_view, key_part, preferred_element_type=jnp.float32
    ) * HEAD_DIM ** (-0.5)
    scores = jnp.where(allowed[:, None], scores, NEGATIVE)
    new_top = jnp.maximum(top_score, jnp.max(scores, axis=-1))
    shrink = jnp.exp(top_score - new_top)
    weights = jnp.where(allowed[:, None], jnp.exp(scores - new_top[..., None]), 0.0)
    sum_weight = sum_weight * shrink + jnp.sum(weights, axis=-1)
    accumulated = accumulated * shrink[..., None] + jnp.einsum(
        "hgsk,khd->hgsd",
        weights.astype(jnp.bfloat16),
        value_part,
        preferred_element_type=jnp.float32,
    )
    return (new_top, sum_weight, accumulated)


def on_device(queries, keys, values, vertical, slash, out_weight):
    row_count = queries.shape[0]
    kv_local = vertical.shape[0]
    chosen_count = vertical.shape[1]
    per_group = queries.shape[1] // (kv_local * HEAD_DIM)
    slab_blocks = row_count // BLK
    my_slab = lax.axis_index("seq")
    first_block = my_slab * slab_blocks
    block_ids = first_block + jnp.arange(slab_blocks, dtype=jnp.int32)
    query_view = queries.reshape(row_count, kv_local, per_group, HEAD_DIM)
    key_view = keys.reshape(row_count, kv_local, HEAD_DIM)
    value_view = values.reshape(row_count, kv_local, HEAD_DIM)
    running = (
        jnp.full((kv_local, per_group, row_count), NEGATIVE, jnp.float32),
        jnp.zeros((kv_local, per_group, row_count), jnp.float32),
        jnp.zeros((kv_local, per_group, row_count, HEAD_DIM), jnp.float32),
    )

    def on_slash(distance):
        return jnp.any(slash[:, None, None, :] == distance[..., None], axis=-1)

    local_blocks = jnp.arange(slab_blocks, dtype=jnp.int32)
    block_gap = local_blocks[:, None] - local_blocks[None, :]
    prev_keys, prev_values = from_behind((keys, values), "seq", 1)
    prev_allowed = spread(on_slash(block_gap + slab_blocks) & (my_slab > 0))
    running = attend(
        running,
        query_view,
        prev_keys.reshape(row_count, kv_local, HEAD_DIM),
        prev_values.reshape(row_count, kv_local, HEAD_DIM),
        prev_allowed,
    )
    token_ids = jnp.arange(row_count)
    causal = token_ids[None, :] <= token_ids[:, None]
    same_block = jnp.broadcast_to(block_gap == 0, (kv_local, slab_blocks, slab_blocks))
    own_allowed = spread(on_slash(block_gap)) | spread(same_block) & causal[None]
    running = attend(running, query_view, key_view, value_view, own_allowed)
    holder_slab = vertical // slab_blocks
    earlier = jnp.arange(chosen_count)[None, :] < jnp.arange(chosen_count)[:, None]
    owner_rank = jnp.sum(
        (holder_slab[:, :, None] == holder_slab[:, None, :]) & earlier[None], axis=-1
    )

    def slot_table(slots):
        holder = slots // CAP
        slot_place = slots % CAP
        matches = (holder_slab[:, None, :] == holder[None, :, None]) & (
            owner_rank[:, None, :] == slot_place[None, :, None]
        )
        return (
            jnp.sum(jnp.where(matches, vertical[:, None, :], 0), axis=-1),
            jnp.any(matches, axis=-1),
        )

    key_blocks = keys.reshape(slab_blocks, BLK, kv_local, HEAD_DIM)
    value_blocks = values.reshape(slab_blocks, BLK, kv_local, HEAD_DIM)
    my_blocks, holding = slot_table(my_slab * CAP + jnp.arange(CAP, dtype=jnp.int32))
    picker = jnp.where(holding, my_blocks - first_block, 0).T[:, None, :, None]
    send_keys = jnp.take_along_axis(key_blocks, picker, axis=0)
    send_values = jnp.take_along_axis(value_blocks, picker, axis=0)
    pieces = sent_together((send_keys, send_values), "seq", 0, 1)
    slot_amount = pieces[0].shape[0]
    slot_blocks, present = slot_table(jnp.arange(slot_amount, dtype=jnp.int32))
    current = running
    key_slots = pieces[0]
    value_slots = pieces[1]
    slot_total = key_slots.shape[0]
    group_slots = math.gcd(slot_total, 8)
    group_count = slot_total // group_slots
    key_groups = key_slots.reshape(group_count, group_slots * BLK, kv_local, HEAD_DIM)
    value_groups = value_slots.reshape(group_count, group_slots * BLK, kv_local, HEAD_DIM)
    block_groups = slot_blocks.reshape(kv_local, group_count, group_slots).transpose(1, 0, 2)
    present_groups = present.reshape(kv_local, group_count, group_slots).transpose(1, 0, 2)

    def advance(partial_state, pieces):
        key_group, value_group, block_group, present_group = pieces
        distance = block_ids[None, :, None] - block_group[:, None, :]
        usable = present_group[:, None, :] & (distance > 0) & jnp.logical_not(on_slash(distance))
        return (attend(partial_state, query_view, key_group, value_group, spread(usable)), None)

    current, unused = lax.scan(
        advance, current, (key_groups, value_groups, block_groups, present_groups)
    )
    running = current
    top_score, sum_weight, accumulated = running
    attention = (accumulated / sum_weight[..., None]).astype(jnp.bfloat16)
    attention = attention.transpose(2, 0, 1, 3).reshape(row_count, kv_local * per_group * HEAD_DIM)
    return summed_on_arrival(
        jnp.dot(attention, out_weight, preferred_element_type=jnp.float32).astype(jnp.bfloat16),
        "head",
        0,
    ).astype(jnp.bfloat16)


def solution(mesh):
    placed = (
        P("seq", "head"),
        P("seq", "head"),
        P("seq", "head"),
        P("head", None),
        P("head", None),
        P("head", None),
    )
    return jax.shard_map(
        on_device, mesh=mesh, in_specs=placed, out_specs=P(("seq", "head"), None), check_vma=False
    )
```

profile of v0, /device:TPU:7, one launch (start us, length us, event | category | flops | bytes accessed | tf_op | source)
XLA Modules:
  0.0 314.0 jit_solution(14388449674000722839)
XLA Ops:
  13.9 3.2 %collective-permute-start = (bf16[256,512]{0,1:T(8,128)(2,1)}, bf16[256,512]{0,1:T(8,128)(2,1)}, u32[]{:S(2)}, u32[]{:S(2)}) collective-permute-start(bf16[256,512]{0,1:T(8,128)(2,1)} %copy.77), channel_id=1, source_target_pairs={{0,2},{2,4},{4,6},{6,8},{8,10},{10,12},{12,14},{14,16},{16,18},{18... | collective-permute-start | bytes 786440 | tf_op jit(solution)/shard_map/ppermute | solution.py:19
  17.9 3.2 %collective-permute-start.1 = (bf16[256,512]{0,1:T(8,128)(2,1)}, bf16[256,512]{0,1:T(8,128)(2,1)}, u32[]{:S(2)}, u32[]{:S(2)}) collective-permute-start(bf16[256,512]{0,1:T(8,128)(2,1)} %copy.85), channel_id=1, source_target_pairs={{0,2},{2,4},{4,6},{6,8},{8,10},{10,12},{12,14},{14,16},{16,18},{18... | collective-permute-start | bytes 786440 | tf_op jit(solution)/shard_map/ppermute | solution.py:19
  26.0 2.6 collective-permute-done
  35.2 3.6 %multiply_add_fusion.2 = f32[4,4,256,128]{3,2,1,0:T(8,128)S(1)} fusion(f32[4,4,256,128]{3,2,1,0:T(8,128)S(1)} %fusion.26, bf16[256,4,128,1]{0,2,3,1:T(8,128)(2,1)} %bitcast.43, f32[4,256,256,4]{2,1,3,0:T(8,128)S(1)} %get-tuple-element.164, f32[4,4,256]{2,1,0:T(4,128)S(1)} %get-tuple-element.160, pred[4,256,256]{1,2,0:T(8,128)(4,1)S(1)} %bitcast.176, ...), kind=kOutput, calls=%fused_computation.43 | convolution fusion | flops 275251200 | bytes 8962048 | tf_op jit(solution)/shard_map/hgsk,khd->hgsd/dot_general | solution.py:56
  38.8 82.9 %all-gather.2.cloned.1.call-done = bf16[128,128,4,128]{3,1,0,2:T(8,128)(2,1)} async-done(((bf16[2,128,4,128]{3,1,0,2:T(8,128)(2,1)}), bf16[128,128,4,128]{3,1,0,2:T(8,128)(2,1)}) %all-gather.2.cloned.1.call-update) | async-done | bytes 16777232 | tf_op jit(solution)/shard_map/all_gather | solution.py:24
  121.6 12.8 %fusion.60 = (bf16[128,64,4,128]{3,1,0,2:T(8,128)(2,1)}, bf16[128,64,4,128]{3,1,0,2:T(8,128)(2,1)}) fusion(bf16[128,128,4,128]{3,1,0,2:T(8,128)(2,1)} %all-gather.2.cloned.1.call-done), kind=kLoop, calls=%fused_computation.110 | loop fusion | bytes 33554432 | tf_op jit(solution)/shard_map/slice | solution.py:26
  134.4 153.3 %while.15 = (s32[]{:T(128)}, f32[4,4,256]{2,1,0:T(4,128)S(1)}, f32[4,4,256]{2,1,0:T(4,128)S(1)}, f32[4,4,256,128]{3,2,1,0:T(8,128)S(1)}, pred[16,4,8]{2,1,0:T(4,...) while((s32[]{:T(128)}, f32[4,4,256]{2,1,0:T(4,128)S(1)}, ...), condition=%wide.region_15.17_spmd.clone, body=%wide.region_11.16_spmd.clone.sunk | while | flops 1102062720 | bytes 33852976 | solution.py:145
  135.1 2.5 fusion.76
  137.7 2.1 fusion.77
  139.8 4.1 %multiply_add_fusion.7 = f32[4,4,256,128]{3,2,1,0:T(8,128)S(1)} fusion(f32[4,4,256,128]{3,2,1,0:T(8,128)S(1)} %get-tuple-element.267, f32[4,512,256,4]{2,1,3,0:T(8,128)S(1)} %get-tuple-element.249, f32[4,4,256]{2,1,0:T(4,128)S(1)} %max.20, pred[4,256,512]{1,2,0:T(8,128)(4,1)S(1)} %bitcast.164, f32[4,4,256]{2,1,0:T(4,128)S(1)} %bitcast.185, ...), kind=kOutput, calls=%fused_computation.10.clone.1 | convolution fusion | flops 548405248 | bytes 13664768 | tf_op jit(solution)/shard_map/while/body/eval_jaxpr/hgsk,khd->hgsd/dot_general | solution.py:56
  144.7 2.5 fusion.76
  147.2 2.1 fusion.77
  149.4 4.1 %multiply_add_fusion.7 = f32[4,4,256,128]{3,2,1,0:T(8,128)S(1)} fusion(f32[4,4,256,128]{3,2,1,0:T(8,128)S(1)} %get-tuple-element.267, f32[4,512,256,4]{2,1,3,0:T(8,128)S(1)} %get-tuple-element.249, f32[4,4,256]{2,1,0:T(4,128)S(1)} %max.20, pred[4,256,512]{1,2,0:T(8,128)(4,1)S(1)} %bitcast.164, f32[4,4,256]{2,1,0:T(4,128)S(1)} %bitcast.185, ...), kind=kOutput, calls=%fused_computation.10.clone.1 | convolution fusion | flops 548405248 | bytes 13664768 | tf_op jit(solution)/shard_map/while/body/eval_jaxpr/hgsk,khd->hgsd/dot_general | solution.py:56
  154.3 2.5 fusion.76
  156.8 2.1 fusion.77
  159.0 4.1 %multiply_add_fusion.7 = f32[4,4,256,128]{3,2,1,0:T(8,128)S(1)} fusion(f32[4,4,256,128]{3,2,1,0:T(8,128)S(1)} %get-tuple-element.267, f32[4,512,256,4]{2,1,3,0:T(8,128)S(1)} %get-tuple-element.249, f32[4,4,256]{2,1,0:T(4,128)S(1)} %max.20, pred[4,256,512]{1,2,0:T(8,128)(4,1)S(1)} %bitcast.164, f32[4,4,256]{2,1,0:T(4,128)S(1)} %bitcast.185, ...), kind=kOutput, calls=%fused_computation.10.clone.1 | convolution fusion | flops 548405248 | bytes 13664768 | tf_op jit(solution)/shard_map/while/body/eval_jaxpr/hgsk,khd->hgsd/dot_general | solution.py:56
  163.9 2.5 fusion.76
  166.4 2.1 fusion.77
  168.5 4.1 %multiply_add_fusion.7 = f32[4,4,256,128]{3,2,1,0:T(8,128)S(1)} fusion(f32[4,4,256,128]{3,2,1,0:T(8,128)S(1)} %get-tuple-element.267, f32[4,512,256,4]{2,1,3,0:T(8,128)S(1)} %get-tuple-element.249, f32[4,4,256]{2,1,0:T(4,128)S(1)} %max.20, pred[4,256,512]{1,2,0:T(8,128)(4,1)S(1)} %bitcast.164, f32[4,4,256]{2,1,0:T(4,128)S(1)} %bitcast.185, ...), kind=kOutput, calls=%fused_computation.10.clone.1 | convolution fusion | flops 548405248 | bytes 13664768 | tf_op jit(solution)/shard_map/while/body/eval_jaxpr/hgsk,khd->hgsd/dot_general | solution.py:56
  173.5 2.5 fusion.76
  176.0 2.1 fusion.77
  178.1 4.1 %multiply_add_fusion.7 = f32[4,4,256,128]{3,2,1,0:T(8,128)S(1)} fusion(f32[4,4,256,128]{3,2,1,0:T(8,128)S(1)} %get-tuple-element.267, f32[4,512,256,4]{2,1,3,0:T(8,128)S(1)} %get-tuple-element.249, f32[4,4,256]{2,1,0:T(4,128)S(1)} %max.20, pred[4,256,512]{1,2,0:T(8,128)(4,1)S(1)} %bitcast.164, f32[4,4,256]{2,1,0:T(4,128)S(1)} %bitcast.185, ...), kind=kOutput, calls=%fused_computation.10.clone.1 | convolution fusion | flops 548405248 | bytes 13664768 | tf_op jit(solution)/shard_map/while/body/eval_jaxpr/hgsk,khd->hgsd/dot_general | solution.py:56
  183.1 2.5 fusion.76
  185.6 2.1 fusion.77
  187.7 4.1 %multiply_add_fusion.7 = f32[4,4,256,128]{3,2,1,0:T(8,128)S(1)} fusion(f32[4,4,256,128]{3,2,1,0:T(8,128)S(1)} %get-tuple-element.267, f32[4,512,256,4]{2,1,3,0:T(8,128)S(1)} %get-tuple-element.249, f32[4,4,256]{2,1,0:T(4,128)S(1)} %max.20, pred[4,256,512]{1,2,0:T(8,128)(4,1)S(1)} %bitcast.164, f32[4,4,256]{2,1,0:T(4,128)S(1)} %bitcast.185, ...), kind=kOutput, calls=%fused_computation.10.clone.1 | convolution fusion | flops 548405248 | bytes 13664768 | tf_op jit(solution)/shard_map/while/body/eval_jaxpr/hgsk,khd->hgsd/dot_general | solution.py:56
  192.6 2.5 fusion.76
  197.3 4.1 %multiply_add_fusion.7 = f32[4,4,256,128]{3,2,1,0:T(8,128)S(1)} fusion(f32[4,4,256,128]{3,2,1,0:T(8,128)S(1)} %get-tuple-element.267, f32[4,512,256,4]{2,1,3,0:T(8,128)S(1)} %get-tuple-element.249, f32[4,4,256]{2,1,0:T(4,128)S(1)} %max.20, pred[4,256,512]{1,2,0:T(8,128)(4,1)S(1)} %bitcast.164, f32[4,4,256]{2,1,0:T(4,128)S(1)} %bitcast.185, ...), kind=kOutput, calls=%fused_computation.10.clone.1 | convolution fusion | flops 548405248 | bytes 13664768 | tf_op jit(solution)/shard_map/while/body/eval_jaxpr/hgsk,khd->hgsd/dot_general | solution.py:56
  202.2 2.5 fusion.76
  206.9 4.1 %multiply_add_fusion.7 = f32[4,4,256,128]{3,2,1,0:T(8,128)S(1)} fusion(f32[4,4,256,128]{3,2,1,0:T(8,128)S(1)} %get-tuple-element.267, f32[4,512,256,4]{2,1,3,0:T(8,128)S(1)} %get-tuple-element.249, f32[4,4,256]{2,1,0:T(4,128)S(1)} %max.20, pred[4,256,512]{1,2,0:T(8,128)(4,1)S(1)} %bitcast.164, f32[4,4,256]{2,1,0:T(4,128)S(1)} %bitcast.185, ...), kind=kOutput, calls=%fused_computation.10.clone.1 | convolution fusion | flops 548405248 | bytes 13664768 | tf_op jit(solution)/shard_map/while/body/eval_jaxpr/hgsk,khd->hgsd/dot_general | solution.py:56
  211.8 2.5 fusion.76
  216.5 4.1 %multiply_add_fusion.7 = f32[4,4,256,128]{3,2,1,0:T(8,128)S(1)} fusion(f32[4,4,256,128]{3,2,1,0:T(8,128)S(1)} %get-tuple-element.267, f32[4,512,256,4]{2,1,3,0:T(8,128)S(1)} %get-tuple-element.249, f32[4,4,256]{2,1,0:T(4,128)S(1)} %max.20, pred[4,256,512]{1,2,0:T(8,128)(4,1)S(1)} %bitcast.164, f32[4,4,256]{2,1,0:T(4,128)S(1)} %bitcast.185, ...), kind=kOutput, calls=%fused_computation.10.clone.1 | convolution fusion | flops 548405248 | bytes 13664768 | tf_op jit(solution)/shard_map/while/body/eval_jaxpr/hgsk,khd->hgsd/dot_general | solution.py:56
  221.4 2.5 fusion.76
  223.9 2.1 fusion.77
  226.0 4.1 %multiply_add_fusion.7 = f32[4,4,256,128]{3,2,1,0:T(8,128)S(1)} fusion(f32[4,4,256,128]{3,2,1,0:T(8,128)S(1)} %get-tuple-element.267, f32[4,512,256,4]{2,1,3,0:T(8,128)S(1)} %get-tuple-element.249, f32[4,4,256]{2,1,0:T(4,128)S(1)} %max.20, pred[4,256,512]{1,2,0:T(8,128)(4,1)S(1)} %bitcast.164, f32[4,4,256]{2,1,0:T(4,128)S(1)} %bitcast.185, ...), kind=kOutput, calls=%fused_computation.10.clone.1 | convolution fusion | flops 548405248 | bytes 13664768 | tf_op jit(solution)/shard_map/while/body/eval_jaxpr/hgsk,khd->hgsd/dot_general | solution.py:56
  231.0 2.5 fusion.76
  235.6 4.1 %multiply_add_fusion.7 = f32[4,4,256,128]{3,2,1,0:T(8,128)S(1)} fusion(f32[4,4,256,128]{3,2,1,0:T(8,128)S(1)} %get-tuple-element.267, f32[4,512,256,4]{2,1,3,0:T(8,128)S(1)} %get-tuple-element.249, f32[4,4,256]{2,1,0:T(4,128)S(1)} %max.20, pred[4,256,512]{1,2,0:T(8,128)(4,1)S(1)} %bitcast.164, f32[4,4,256]{2,1,0:T(4,128)S(1)} %bitcast.185, ...), kind=kOutput, calls=%fused_computation.10.clone.1 | convolution fusion | flops 548405248 | bytes 13664768 | tf_op jit(solution)/shard_map/while/body/eval_jaxpr/hgsk,khd->hgsd/dot_general | solution.py:56
  240.6 2.5 fusion.76
  245.2 4.1 %multiply_add_fusion.7 = f32[4,4,256,128]{3,2,1,0:T(8,128)S(1)} fusion(f32[4,4,256,128]{3,2,1,0:T(8,128)S(1)} %get-tuple-element.267, f32[4,512,256,4]{2,1,3,0:T(8,128)S(1)} %get-tuple-element.249, f32[4,4,256]{2,1,0:T(4,128)S(1)} %max.20, pred[4,256,512]{1,2,0:T(8,128)(4,1)S(1)} %bitcast.164, f32[4,4,256]{2,1,0:T(4,128)S(1)} %bitcast.185, ...), kind=kOutput, calls=%fused_computation.10.clone.1 | convolution fusion | flops 548405248 | bytes 13664768 | tf_op jit(solution)/shard_map/while/body/eval_jaxpr/hgsk,khd->hgsd/dot_general | solution.py:56
  250.1 2.5 fusion.76
  254.8 4.1 %multiply_add_fusion.7 = f32[4,4,256,128]{3,2,1,0:T(8,128)S(1)} fusion(f32[4,4,256,128]{3,2,1,0:T(8,128)S(1)} %get-tuple-element.267, f32[4,512,256,4]{2,1,3,0:T(8,128)S(1)} %get-tuple-element.249, f32[4,4,256]{2,1,0:T(4,128)S(1)} %max.20, pred[4,256,512]{1,2,0:T(8,128)(4,1)S(1)} %bitcast.164, f32[4,4,256]{2,1,0:T(4,128)S(1)} %bitcast.185, ...), kind=kOutput, calls=%fused_computation.10.clone.1 | convolution fusion | flops 548405248 | bytes 13664768 | tf_op jit(solution)/shard_map/while/body/eval_jaxpr/hgsk,khd->hgsd/dot_general | solution.py:56
  259.7 2.5 fusion.76
  264.4 4.1 %multiply_add_fusion.7 = f32[4,4,256,128]{3,2,1,0:T(8,128)S(1)} fusion(f32[4,4,256,128]{3,2,1,0:T(8,128)S(1)} %get-tuple-element.267, f32[4,512,256,4]{2,1,3,0:T(8,128)S(1)} %get-tuple-element.249, f32[4,4,256]{2,1,0:T(4,128)S(1)} %max.20, pred[4,256,512]{1,2,0:T(8,128)(4,1)S(1)} %bitcast.164, f32[4,4,256]{2,1,0:T(4,128)S(1)} %bitcast.185, ...), kind=kOutput, calls=%fused_computation.10.clone.1 | convolution fusion | flops 548405248 | bytes 13664768 | tf_op jit(solution)/shard_map/while/body/eval_jaxpr/hgsk,khd->hgsd/dot_general | solution.py:56
  269.3 2.5 fusion.76
  274.0 4.1 %multiply_add_fusion.7 = f32[4,4,256,128]{3,2,1,0:T(8,128)S(1)} fusion(f32[4,4,256,128]{3,2,1,0:T(8,128)S(1)} %get-tuple-element.267, f32[4,512,256,4]{2,1,3,0:T(8,128)S(1)} %get-tuple-element.249, f32[4,4,256]{2,1,0:T(4,128)S(1)} %max.20, pred[4,256,512]{1,2,0:T(8,128)(4,1)S(1)} %bitcast.164, f32[4,4,256]{2,1,0:T(4,128)S(1)} %bitcast.185, ...), kind=kOutput, calls=%fused_computation.10.clone.1 | convolution fusion | flops 548405248 | bytes 13664768 | tf_op jit(solution)/shard_map/while/body/eval_jaxpr/hgsk,khd->hgsd/dot_general | solution.py:56
  278.9 2.5 fusion.76
  283.5 4.1 %multiply_add_fusion.7 = f32[4,4,256,128]{3,2,1,0:T(8,128)S(1)} fusion(f32[4,4,256,128]{3,2,1,0:T(8,128)S(1)} %get-tuple-element.267, f32[4,512,256,4]{2,1,3,0:T(8,128)S(1)} %get-tuple-element.249, f32[4,4,256]{2,1,0:T(4,128)S(1)} %max.20, pred[4,256,512]{1,2,0:T(8,128)(4,1)S(1)} %bitcast.164, f32[4,4,256]{2,1,0:T(4,128)S(1)} %bitcast.185, ...), kind=kOutput, calls=%fused_computation.10.clone.1 | convolution fusion | flops 548405248 | bytes 13664768 | tf_op jit(solution)/shard_map/while/body/eval_jaxpr/hgsk,khd->hgsd/dot_general | solution.py:56
  291.2 8.4 %convolution_convert_fusion = bf16[256,4096]{1,0:T(8,128)(2,1)S(1)} fusion(bf16[256,2048]{0,1:T(8,128)(2,1)S(1)} %bitcast.172, bf16[2048,4096]{1,0:T(8,128)(2,1)} %param.15), kind=kOutput, calls=%fused_computation.29 | convolution fusion | flops 4296015872 | bytes 19922944 | tf_op jit(solution)/shard_map/dot_general | solution.py:153
  299.7 5.9 %all_to_all.5 = bf16[2,128,4096]{2,1,0:T(8,128)(2,1)S(1)} all-to-all(bf16[2,128,4096]{2,1,0:T(8,128)(2,1)S(1)} %bitcast.169), channel_id=1, replica_groups=mesh['seq'=64,'head'=2] {'head'}, dimensions={0} | all-to-all | bytes 4194304 | tf_op jit(solution)/shard_map/all_to_all | solution.py:38
  (291 shorter events, 55.2 us)
Async XLA Ops:
  6.5 17.2 %copy-start.5 = (s32[4,64]{1,0:T(4,128)S(1)}, s32[4,64]{1,0:T(4,128)}, u32[]{:S(2)}) copy-start(s32[4,64]{1,0:T(4,128)} %param.13) | copy-start | bytes 3076
  6.5 6.5 %copy-start = (bf16[256,512]{1,0:T(8,128)(2,1)S(1)}, bf16[256,512]{1,0:T(8,128)(2,1)}, u32[]{:S(2)}) copy-start(bf16[256,512]{1,0:T(8,128)(2,1)} %param.11) | copy-start | bytes 786436
  6.5 10.5 %copy-start.1 = (bf16[256,512]{1,0:T(8,128)(2,1)S(1)}, bf16[256,512]{1,0:T(8,128)(2,1)}, u32[]{:S(2)}) copy-start(bf16[256,512]{1,0:T(8,128)(2,1)} %param.12) | copy-start | bytes 786436
  6.5 15.5 %copy-start.6 = (s32[4,2]{0,1:T(2,128)S(1)}, s32[4,2]{0,1:T(2,128)}, u32[]{:S(2)}) copy-start(s32[4,2]{0,1:T(2,128)} %param.14) | copy-start | bytes 100
  6.5 16.0 %copy-start.3 = (bf16[256,2048]{1,0:T(8,128)(2,1)S(1)}, bf16[256,2048]{1,0:T(8,128)(2,1)}, u32[]{:S(2)}) copy-start(bf16[256,2048]{1,0:T(8,128)(2,1)} %param.10) | copy-start | bytes 3145732
  6.5 115.1 %all-gather.2.cloned.1.call-start = ((), (), s32[]{:S(2)}) async-start(), calls=%async_computation.1 | async-start | bytes 17039360 | tf_op jit(solution)/shard_map/all_gather | solution.py:24
  13.9 14.7 %collective-permute-start = (bf16[256,512]{0,1:T(8,128)(2,1)}, bf16[256,512]{0,1:T(8,128)(2,1)}, u32[]{:S(2)}, u32[]{:S(2)}) collective-permute-start(bf16[256,512]{0,1:T(8,128)(2,1)} %copy.77), channel_id=1, source_target_pairs={{0,2},{2,4},{4,6},{6,8},{8,10},{10,12},{12,14},{14,16},{16,18},{18... | collective-permute-start | bytes 786440 | tf_op jit(solution)/shard_map/ppermute | solution.py:19
  17.9 17.2 %collective-permute-start.1 = (bf16[256,512]{0,1:T(8,128)(2,1)}, bf16[256,512]{0,1:T(8,128)(2,1)}, u32[]{:S(2)}, u32[]{:S(2)}) collective-permute-start(bf16[256,512]{0,1:T(8,128)(2,1)} %copy.85), channel_id=1, source_target_pairs={{0,2},{2,4},{4,6},{6,8},{8,10},{10,12},{12,14},{14,16},{16,18},{18... | collective-permute-start | bytes 786440 | tf_op jit(solution)/shard_map/ppermute | solution.py:19
  28.6 3.0 copy-start.4
  287.7 1.4 copy-start.2
Sparse Core Ops, SparseCore 0:
  13.2 108.4 all-gather.1
where the time goes:
time: 316 us; the launch traced here: 314 us
  matrix products  122 us (39%)
  waiting for transfers between devices  86.4 us (27%)
  other arithmetic  45.4 us (14%)
  local copies, waits for them, and re-layouts  32.1 us (10%)
  between operations  13.7 us (4%)
  starting transfers between devices  6.43 us (2%)
  blocking collectives  5.89 us (2%)
    all_gather x1, waiting for transfers between devices, sent_together(): lax.all_gather(both, axis, axis=dim, tiled=True)  82.9 us
    dot_general x18, matrix products, attend(): jnp.einsum('hgsk,khd->hgsd', weights.astype(jnp.bfloat16), value_part, pr...  71.2 us
    dot_general x18, matrix products, attend(): jnp.einsum('shgd,khd->hgsk', query_view, key_part, preferred_element_type...  42.8 us
    reduce_sum x18, other arithmetic, attend(): sum_weight = sum_weight * shrink + jnp.sum(weights, axis=-1)  35.9 us
    slice x1, local copies, waits for them, and re-layouts, sent_together(): lax.slice_in_dim(filled, at, at + a.shape[along], axis=along)  12.8 us
    dot_general x1, matrix products, on_device(): jnp.dot(attention, out_weight, preferred_element_type=jnp.float32)  8.44 us
    ppermute x2, starting transfers between devices, from_behind(): return lax.ppermute(shard, axis, pairs)  6.39 us
  transfers between devices with their start and end apart: 3, of which 3 were waited for; matrix products, arithmetic and copies ran while one was open for 5% of the time, Pallas kernels for 0%

commit v1 on v0

v1 whole, which is shorter than its diff:
```python
import functools
import math

import jax
import jax.numpy as jnp
from jax import lax
from jax.experimental import pallas as pl
from jax.experimental.pallas import tpu as pltpu
from jax.sharding import PartitionSpec as P

D = 128
BLK = 64
CAP = 2
KVL = 4
G = 4
ROWS = 256
NB = 4
RING = 4
PLANE = 16
NV = 64
OUT = 4096
NEG = -1e30
C2 = D**-0.5 * math.log2(math.e)
MESH = pl.DeviceIdType.MESH
CHUNK = 8


def dot_t(a, b):
    return lax.dot_general(a, b, (((1,), (1,)), ((), ())), preferred_element_type=jnp.float32)


def dot_n(a, b):
    return lax.dot_general(a, b, (((1,), (0,)), ((), ())), preferred_element_type=jnp.float32)


DIRS = {"y+": (0, 1), "y-": (0, -1), "z+": (1, 0), "z-": (-1, 0)}


def plan():
    moves, waits = [], []

    def add(dz, dy, x0, nx, way):
        moves.append((dz, dy, x0, nx, way))
        return len(moves) - 1

    steps = []
    own = {w: add(0, 0, 0, 4, w) for w in ("y-", "z-", "z+", "y+")}
    steps.append(([], list(own.values())))
    up = [add(0, 1, 0, 4, "y-"), add(0, 1, 0, 2, "z+"), add(0, 1, 0, 2, "z-")]
    steps.append(([own["y-"]], up))
    zu = [add(1, 0, 2, 1, "z-"), add(1, 0, 0, 1, "z-"), add(1, 0, 2, 2, "y-"), add(1, 0, 2, 2, "y+")]
    steps.append(([own["z-"]], zu))
    zd = [add(-1, 0, 3, 1, "z+"), add(-1, 0, 1, 1, "z+"), add(-1, 0, 2, 2, "y-"), add(-1, 0, 2, 2, "y+")]
    steps.append(([own["z+"]], zd))
    dn = [add(0, -1, 0, 2, "z+"), add(0, -1, 0, 2, "z-")]
    steps.append(([own["y+"]], dn))
    z2 = [add(2, 0, 2, 2, "y-"), add(2, 0, 2, 2, "y+")]
    steps.append(([zu[0], zd[0]], z2))
    y2 = [add(0, 2, 0, 2, "z+"), add(0, 2, 0, 2, "z-")]
    steps.append(([up[0]], y2))
    a_in = {1: (up[1], up[2]), -1: (dn[0], dn[1]), 2: (y2[0], y2[1])}
    b_in = {1: (zu[2], zu[3]), -1: (zd[2], zd[3]), 2: (z2[0], z2[1])}
    last = [zu[1], zd[1]]
    for d in (1, -1, 2):
        plus, minus = a_in[d]
        f = add(1, d, 0, 1, "z-")
        steps.append(([minus], [f]))
        g = add(-1, d, 1, 1, "z+")
        steps.append(([plus], [g]))
        bm, bp = b_in[d]
        h = add(d, 1, 2, 2, "y-")
        steps.append(([bm], [h]))
        last += [f, g, h, bp]
    steps.append((last, []))
    return moves, steps


MOVES, STEPS = plan()


def exchange_kernel(
    vert, slash, q_ref, k_ref, v_ref, kv_out, qx_out, ol_ref, ll_ref,
    kvb, qx, sel, prev, bias,
    x_send, x_recv, q_send, q_recv, p_send, p_recv, m_send, m_recv, out_sem,
):
    s = lax.axis_index("seq")
    core = lax.axis_index("head")
    x, z, y = s // 16, (s // 4) % 4, s % 4
    p = s % 16

    def at(ax, az, ay):
        return (ax % 4) * 16 + (az % 4) * 4 + ay % 4

    right, left = (s + 1) % 64, (s + 63) % 64
    x_peers = [at(x + d, z, y) for d in (1, 2, 3)]
    greet = x_peers + [at(x, z + dz, y + dy) for dz, dy in DIRS.values()] + [right, left]
    barrier = pltpu.get_barrier_semaphore()
    for peer in greet:
        pl.semaphore_signal(barrier, inc=1, device_id=(peer, core), device_id_type=MESH)

    for h in range(KVL):
        def scan(r, found):
            count, first, second = found
            inside = vert[h, r] - s * NB
            here = jnp.where((inside >= 0) & (inside < NB), 1, 0)
            first = first + here * jnp.where(count == 0, inside, 0)
            second = second + here * jnp.where(count == 1, inside, 0)
            return count + here, first, second

        zero = jnp.int32(0)
        unused, first, second = lax.fori_loop(0, NV, scan, (zero, zero, zero), unroll=8)
        cols = slice(h * D, (h + 1) * D)
        for slot, b in enumerate((first, second)):
            for far, ref in ((0, k_ref), (2, v_ref)):
                picked = jnp.zeros((BLK, D), jnp.float32)
                for i in range(NB):
                    block = ref[i * BLK : (i + 1) * BLK, cols].astype(jnp.float32)
                    picked = picked + block * jnp.where(b == i, 1.0, 0.0)
                sel[h, far + slot] = picked.astype(jnp.bfloat16)
    kvb[p, x] = sel[x]
    pl.semaphore_wait(barrier, len(greet))

    def remote(src, dst, a, b, peer):
        return pltpu.make_async_remote_copy(
            src_ref=src, dst_ref=dst, send_sem=a, recv_sem=b,
            device_id=(peer, core), device_id_type=MESH,
        )

    x_copies = [
        remote(sel.at[(x + d) % 4], kvb.at[p, x], x_send.at[d - 1], x_recv.at[d - 1], x_peers[d - 1])
        for d in (1, 2, 3)
    ]
    for d in (2, 1, 3):
        x_copies[d - 1].start()
    p_copies = [
        remote(ref, prev.at[i], p_send.at[i], p_recv.at[i], right)
        for i, ref in enumerate((k_ref, v_ref))
    ]
    p_copies[0].start()
    q_copies = [
        remote(
            q_ref.at[:, pl.ds(pl.multiple_of(((x + d) % 4) * (G * D), G * D), G * D)],
            qx.at[x], q_send.at[d - 1], q_recv.at[d - 1], x_peers[d - 1],
        )
        for d in (1, 2, 3)
    ]
    for d in (2, 1, 3):
        q_copies[d - 1].start()
    qx[x] = q_ref[:, pl.ds(pl.multiple_of(x * (G * D), G * D), G * D)]

    moves = []
    for i, (dz, dy, x0, nx, way) in enumerate(MOVES):
        wz, wy = DIRS[way]
        piece = kvb.at[((z + dz) % 4) * 4 + (y + dy) % 4, pl.ds(x0, nx)]
        moves.append(remote(piece, piece, m_send.at[i], m_recv.at[i], at(x, z + wz, y + wy)))

    key_block = lax.broadcasted_iota(jnp.int32, (8, 2 * ROWS), 1) // BLK
    block_id = key_block + (s - 1) * NB
    for h in range(KVL):
        def mark(r, seen):
            return seen | jnp.where(block_id == vert[h, r], 1, 0)

        seen = lax.fori_loop(0, NV, mark, jnp.zeros((8, 2 * ROWS), jnp.int32), unroll=8)
        gap = lax.broadcasted_iota(jnp.int32, (8, 2 * ROWS), 0) + NB - key_block
        near = (gap == 0) | (gap == slash[h, 0]) | (gap == slash[h, 1]) | (seen > 0)
        ok = near & (gap >= 0) & (block_id >= 0)
        bias[h] = jnp.where(ok, 0.0, NEG)

    def local_unit(h, a):
        keys = 2 * ROWS if a >= 2 else ROWS + 2 * BLK
        own_keys = keys - ROWS
        cols = slice(h * D, (h + 1) * D)
        rows = slice(a * BLK, (a + 1) * BLK)
        q = jnp.concatenate(
            [q_ref[rows, (h * G + g) * D : (h * G + g + 1) * D] for g in range(G)], axis=0
        )
        ks = jnp.concatenate([prev[0, :, cols], k_ref[:own_keys, cols]], axis=0)
        vs = jnp.concatenate([prev[1, :, cols], v_ref[:own_keys, cols]], axis=0)
        t = lax.broadcasted_iota(jnp.int32, (G * BLK, keys), 0) % BLK + (ROWS + a * BLK)
        u = lax.broadcasted_iota(jnp.int32, (G * BLK, keys), 1)
        scores = dot_t(q, ks) + bias[h, a : a + 1, :keys]
        scores = jnp.where(u <= t, scores, NEG)
        top = jnp.max(scores, axis=1, keepdims=True)
        weights = jnp.exp2((scores - top) * C2)
        total = jnp.sum(weights, axis=1, keepdims=True)
        out = dot_n(weights.astype(jnp.bfloat16), vs) / total
        level = top * C2 + jnp.log2(total)
        lane = lax.broadcasted_iota(jnp.int32, (BLK, D), 1)
        levels = ll_ref[rows, :] if h else jnp.zeros((BLK, D), jnp.float32)
        for g in range(G):
            part = slice(g * BLK, (g + 1) * BLK)
            ol_ref[rows, (h * G + g) * D : (h * G + g + 1) * D] = out[part]
            levels = jnp.where(lane == h * G + g, level[part], levels)
        ll_ref[rows, :] = levels

    units = [(h, a) for a in range(NB) for h in range(KVL)]

    for c in x_copies:
        c.wait_recv()
    for i, (need, begin) in enumerate(STEPS):
        for w in need:
            moves[w].wait_recv()
        for w in begin:
            moves[w].start()
        if i == 0:
            p_copies[1].start()
        if i == 6:
            for c in p_copies:
                c.wait_recv()
        if i >= 6:
            for unused in range(2):
                if units:
                    local_unit(*units.pop(0))
    while units:
        local_unit(*units.pop(0))
    for c in q_copies:
        c.wait_recv()
    outs = [
        pltpu.make_async_copy(kvb, kv_out, out_sem.at[0]),
        pltpu.make_async_copy(qx, qx_out, out_sem.at[1]),
    ]
    for c in outs:
        c.start()
    for c in x_copies + q_copies + p_copies + moves:
        c.wait_send()
    for c in outs:
        c.wait()


def exchange(vertical, slash, queries, keys, values):
    bf16, f32 = jnp.bfloat16, jnp.float32
    vmem = pl.BlockSpec(memory_space=pltpu.VMEM)
    smem = pl.BlockSpec(memory_space=pltpu.SMEM)
    hbm = pl.BlockSpec(memory_space=pl.ANY)
    dma = pltpu.SemaphoreType.DMA
    n = len(MOVES)
    return pl.pallas_call(
        exchange_kernel,
        out_shape=(
            jax.ShapeDtypeStruct((PLANE, RING, 2 * CAP, BLK, D), bf16),
            jax.ShapeDtypeStruct((RING, ROWS, G * D), bf16),
            jax.ShapeDtypeStruct((ROWS, KVL * G * D), f32),
            jax.ShapeDtypeStruct((ROWS, D), f32),
        ),
        in_specs=[smem, smem, vmem, vmem, vmem],
        out_specs=(hbm, hbm, vmem, vmem),
        scratch_shapes=[
            pltpu.VMEM((PLANE, RING, 2 * CAP, BLK, D), bf16),
            pltpu.VMEM((RING, ROWS, G * D), bf16),
            pltpu.VMEM((RING, 2 * CAP, BLK, D), bf16),
            pltpu.VMEM((2, ROWS, KVL * D), bf16),
            pltpu.VMEM((KVL, 8, 2 * ROWS), f32),
            dma((3,)), dma((3,)), dma((3,)), dma((3,)), dma((2,)), dma((2,)),
            dma((n,)), dma((n,)), dma((2,)),
        ],
        compiler_params=pltpu.CompilerParams(collective_id=0, has_side_effects=True),
        name="exchange",
    )(vertical, slash, queries, keys, values)


def vertical_kernel(vert, kv_ref, qx_ref, ov_ref, lv_ref, kc, vc, m_ref, l_ref, acc, sems):
    s = lax.axis_index("seq")
    x, p = s // 16, s % 16
    step = CHUNK * BLK

    def fetch(r):
        b = vert[x, r]
        slab = b // NB
        before = vert[x, jnp.maximum(r - 1, 0)] // NB
        slot = jnp.where((r > 0) & (before == slab), 1, 0)
        rows = pl.ds(pl.multiple_of(r * BLK, BLK), BLK)
        src = kv_ref.at[slab % 16, slab // 16]
        return (
            pltpu.make_async_copy(src.at[slot], kc.at[rows], sems.at[0, r // CHUNK]),
            pltpu.make_async_copy(src.at[2 + slot], vc.at[rows], sems.at[1, r // CHUNK]),
        )

    def begin(r, unused):
        for c in fetch(r):
            c.start()
        return unused

    lax.fori_loop(0, NV, begin, 0)

    def count(i):
        limit = (i * 16 + p - 1) * NB
        return lax.fori_loop(
            0, NV, lambda r, n: n + jnp.where(vert[x, r] < limit, 1, 0), jnp.int32(0), unroll=8
        )

    for c in range(NV // CHUNK):
        rows = pl.ds(c * step, step)
        pltpu.make_async_copy(kc.at[rows], kc.at[rows], sems.at[0, c]).wait()
        pltpu.make_async_copy(vc.at[rows], vc.at[rows], sems.at[1, c]).wait()

    def slab_step(i, unused):
        n = count(i)
        full = n // CHUNK
        m_ref[...] = jnp.full(m_ref.shape, NEG, jnp.float32)
        l_ref[...] = jnp.zeros(l_ref.shape, jnp.float32)
        acc[...] = jnp.zeros(acc.shape, jnp.float32)

        def chunk(c, masked):
            rows = pl.ds(pl.multiple_of(c * step, step), step)
            ks, vs = kc[rows, :], vc[rows, :]
            for g in range(G):
                q = qx_ref[i, :, g * D : (g + 1) * D]
                scores = dot_t(q, ks)
                if masked:
                    u = lax.broadcasted_iota(jnp.int32, (1, step), 1) + c * step
                    scores = jnp.where(u < n * BLK, scores, NEG)
                old = m_ref[g]
                top = jnp.maximum(old, jnp.max(scores, axis=1, keepdims=True))
                shrink = jnp.exp2((old - top) * C2)
                weights = jnp.exp2((scores - top[:, :1]) * C2)
                l_ref[g] = l_ref[g] * shrink + jnp.sum(weights, axis=1, keepdims=True)
                acc[g] = acc[g] * shrink + dot_n(weights.astype(jnp.bfloat16), vs)
                m_ref[g] = top

        lax.fori_loop(0, full, lambda c, u: (chunk(c, False), u)[1], 0)

        @pl.when(full * CHUNK < n)
        def _():
            chunk(full, True)

        lane = lax.broadcasted_iota(jnp.int32, (ROWS, D), 1)
        levels = jnp.full((ROWS, D), NEG, jnp.float32)
        for g in range(G):
            total = l_ref[g]
            some = total > 0.0
            safe = jnp.where(some, total, 1.0)
            ov_ref[i, :, g * D : (g + 1) * D] = (acc[g] / safe).astype(jnp.bfloat16)
            level = jnp.where(some, m_ref[g] * C2 + jnp.log2(safe), NEG)
            levels = jnp.where(lane == g, level, levels)
        lv_ref[i] = levels.T[:8, :]
        return unused

    lax.fori_loop(0, RING, slab_step, 0)


def vertical_part(vertical, kv, qx):
    bf16, f32 = jnp.bfloat16, jnp.float32
    vmem = pl.BlockSpec(memory_space=pltpu.VMEM)
    return pl.pallas_call(
        vertical_kernel,
        out_shape=(
            jax.ShapeDtypeStruct((RING, ROWS, G * D), bf16),
            jax.ShapeDtypeStruct((RING, 8, ROWS), f32),
        ),
        in_specs=[
            pl.BlockSpec(memory_space=pltpu.SMEM), pl.BlockSpec(memory_space=pl.ANY), vmem,
        ],
        out_specs=(vmem, vmem),
        scratch_shapes=[
            pltpu.VMEM((NV * BLK, D), bf16),
            pltpu.VMEM((NV * BLK, D), bf16),
            pltpu.VMEM((G, ROWS, D), f32),
            pltpu.VMEM((G, ROWS, D), f32),
            pltpu.VMEM((G, ROWS, D), f32),
            pltpu.SemaphoreType.DMA((2, NV // CHUNK)),
        ],
        name="verticals",
    )(vertical, kv, qx)


def project_kernel(
    ov_ref, lv_ref, ol_ref, ll_ref, w_hbm, out_ref,
    w, ovb, lvb, att, acc, give, take,
    w_sem, o_send, o_recv, l_send, l_recv, c_send, c_recv,
):
    s = lax.axis_index("seq")
    core = lax.axis_index("head")
    x, p = s // 16, s % 16
    peers = [((x + d) % 4) * 16 + p for d in (1, 2, 3)]
    barrier = pltpu.get_barrier_semaphore()
    for peer in peers:
        pl.semaphore_signal(barrier, inc=1, device_id=(peer, core), device_id_type=MESH)
    pl.semaphore_signal(barrier, inc=1, device_id=(s, 1 - core), device_id_type=MESH)

    order = [(x + d) % 4 for d in (0, 1, 3, 2)]
    w_copies = []
    for i, h in enumerate(order):
        rows = pl.ds(pl.multiple_of(h * (G * D), G * D), G * D)
        c = pltpu.make_async_copy(w_hbm.at[rows], w.at[i], w_sem.at[i])
        c.start()
        w_copies.append(c)
    pl.semaphore_wait(barrier, 4)

    def remote(src, dst, a, b, peer):
        return pltpu.make_async_remote_copy(
            src_ref=src, dst_ref=dst, send_sem=a, recv_sem=b,
            device_id=peer, device_id_type=MESH,
        )

    copies = {}
    for d in (2, 1, 3):
        to = (x + d) % 4
        copies[d] = (
            remote(lv_ref.at[to], lvb.at[x], l_send.at[d - 1], l_recv.at[d - 1], (peers[d - 1], core)),
            remote(ov_ref.at[to], ovb.at[x], o_send.at[d - 1], o_recv.at[d - 1], (peers[d - 1], core)),
        )
        for c in copies[d]:
            c.start()

    def merge(h, ov, lv):
        level = jnp.concatenate([lv, jnp.full((D - 8, ROWS), NEG, jnp.float32)], axis=0).T
        base = ll_ref[...]
        lane = lax.broadcasted_iota(jnp.int32, (ROWS, D), 1)
        for g in range(G):
            mine = jnp.sum(jnp.where(lane == h * G + g, base, 0.0), axis=1, keepdims=True)
            far = level[:, g : g + 1]
            share = 1.0 / (1.0 + jnp.exp2(far - mine))
            cols = pl.ds(pl.multiple_of((h * G + g) * D, D), D)
            v = ov[:, g * D : (g + 1) * D].astype(jnp.float32)
            mixed = ol_ref[:, cols] * share + v * (1.0 - share)
            att[:, g * D : (g + 1) * D] = mixed.astype(jnp.bfloat16)

    tile = 512

    def part(i, rows, cols):
        return dot_n(att[rows, :], w[i, :, cols])

    everything = pl.ds(0, ROWS)
    for i, d in enumerate((0, 1, 3)):
        h = order[i]
        if d == 0:
            merge(h, ov_ref[x], lv_ref[x])
        else:
            for c in copies[4 - d]:
                c.wait_recv()
            merge(h, ovb[h], lvb[h])
        w_copies[i].wait()

        @pl.loop(0, OUT // tile)
        def _(t):
            cols = pl.ds(pl.multiple_of(t * tile, tile), tile)
            if i == 0:
                acc[:, cols] = part(i, everything, cols)
            else:
                acc[:, cols] += part(i, everything, cols)

    h = order[3]
    for c in copies[2]:
        c.wait_recv()
    merge(h, ovb[h], lvb[h])
    w_copies[3].wait()
    half = ROWS // 2
    theirs = pl.ds(pl.multiple_of((1 - core) * half, half), half)
    mine = pl.ds(pl.multiple_of(core * half, half), half)
    wide = 1024
    handed = []
    for t in range(OUT // wide):
        cols = pl.ds(t * wide, wide)
        give[t] = (acc[theirs, cols] + part(3, theirs, cols)).astype(jnp.bfloat16)
        c = remote(give.at[t], take.at[t], c_send.at[t], c_recv.at[t], (s, 1 - core))
        c.start()
        handed.append(c)
    for t in range(OUT // wide):
        cols = pl.ds(t * wide, wide)
        total = acc[mine, cols] + part(3, mine, cols)
        handed[t].wait_recv()
        out_ref[:, cols] = (total + take[t].astype(jnp.float32)).astype(jnp.bfloat16)
    for d in (1, 2, 3):
        for c in copies[d]:
            c.wait_send()
    for c in handed:
        c.wait_send()


def project(ov, lv, ol, ll, out_weight):
    bf16, f32 = jnp.bfloat16, jnp.float32
    vmem = pl.BlockSpec(memory_space=pltpu.VMEM)
    dma = pltpu.SemaphoreType.DMA
    return pl.pallas_call(
        project_kernel,
        out_shape=jax.ShapeDtypeStruct((ROWS // 2, OUT), bf16),
        in_specs=[vmem, vmem, vmem, vmem, pl.BlockSpec(memory_space=pl.ANY)],
        out_specs=vmem,
        scratch_shapes=[
            pltpu.VMEM((KVL, G * D, OUT), bf16),
            pltpu.VMEM((RING, ROWS, G * D), bf16),
            pltpu.VMEM((RING, 8, ROWS), f32),
            pltpu.VMEM((ROWS, G * D), bf16),
            pltpu.VMEM((ROWS, OUT), f32),
            pltpu.VMEM((4, ROWS // 2, 1024), bf16),
            pltpu.VMEM((4, ROWS // 2, 1024), bf16),
            dma((4,)), dma((3,)), dma((3,)), dma((3,)), dma((3,)), dma((4,)), dma((4,)),
        ],
        compiler_params=pltpu.CompilerParams(collective_id=1, has_side_effects=True),
        name="project",
    )(ov, lv, ol, ll, out_weight)


def on_device(queries, keys, values, vertical, slash, out_weight):
    kv, qx, ol, ll = exchange(vertical, slash, queries, keys, values)
    ov, lv = vertical_part(vertical, kv, qx)
    return project(ov, lv, ol, ll, out_weight)


def solution(mesh):
    placed = (
        P("seq", "head"),
        P("seq", "head"),
        P("seq", "head"),
        P("head", None),
        P("head", None),
        P("head", None),
    )
    return jax.shard_map(
        on_device, mesh=mesh, in_specs=placed, out_specs=P(("seq", "head"), None), check_vma=False
    )
```

time: 316 us -> 139 us (0.44)
  the two profiles are of different devices: /device:TPU:7 before, /device:TPU:121 now
where the time goes in v1:
time: 139 us
  Pallas kernels  135 us (97%)
  local copies, waits for them, and re-layouts  3.62 us (3%)
    pallas_call x1, Pallas kernels, vertical_part(): pl.pallas_call(vertical_kernel, out_shape=(jax.ShapeDtypeStruct((RING, RO...  57.2 us
    pallas_call x1, Pallas kernels, exchange(): pl.pallas_call(exchange_kernel, out_shape=(jax.ShapeDtypeStruct((PLANE, R...  42.1 us
    pallas_call x1, Pallas kernels, project(): pl.pallas_call(project_kernel, out_shape=jax.ShapeDtypeStruct((ROWS // 2,...  35.6 us
    unnamed x2, local copies, waits for them, and re-layouts  3.62 us

profile of v1, /device:TPU:121, one launch (start us, length us, event | category | flops | bytes accessed | tf_op | source)
XLA Modules:
  0.0 138.5 jit_solution(11171733398653995919)
XLA Ops:
  0.0 1.3 copy.7.slash
  1.3 42.1 %exchange.1 = (bf16[16,4,4,64,128]{4,3,2,1,0:T(8,128)(2,1)}, bf16[4,256,512]{2,1,0:T(8,128)(2,1)}, f32[256,2048]{1,0:T(8,128)}, f32[256,128]{1,0:T(8,128)}) custom-call(s32[4,64]{1,0:T(4,128)} %vert.3, s32[4,2]{1,0:T(4,128)} %copy.7.slash, bf16[256,2048]{1,0:T(8,128)(2,1)} %q_ref.1, bf16[256,512]{1,0:T(8,128)(2,1)} %k_ref.1, bf16[256,512]{1,0:T(8,128)(2,1)} %v_ref.1), custom_call_target="tpu_custom_call" | custom-call | tf_op jit(solution)/shard_map/exchange/pallas_call | solution.py:237
  43.5 57.2 %verticals.1 = (bf16[4,256,512]{2,1,0:T(8,128)(2,1)}, f32[4,8,256]{2,1,0:T(8,128)}) custom-call(s32[4,64]{1,0:T(4,128)} %vert.3, bf16[16,4,4,64,128]{4,3,2,1,0:T(8,128)(2,1)} %get-tuple-element.11.kv_ref, bf16[4,256,512]{2,1,0:T(8,128)(2,1)} %get-tuple-element.12.qx_ref), custom_call_target="tpu_custom_call" | custom-call | tf_op jit(solution)/shard_map/verticals/pallas_call | solution.py:344
  100.6 35.6 %project.1 = bf16[128,4096]{1,0:T(8,128)(2,1)} custom-call(bf16[4,256,512]{2,1,0:T(8,128)(2,1)} %get-tuple-element.13.ov_ref, f32[4,8,256]{2,1,0:T(8,128)} %get-tuple-element.14.lv_ref, f32[256,2048]{1,0:T(8,128)} %get-tuple-element.15.ol_ref, f32[256,128]{1,0:T(8,128)} %get-tuple-element.16.ll_ref, bf16[2048,4096]{1,0:T(8,128)(2,1)} %w_hbm.1), custom_call_target="tpu_custom_call" | custom-call | tf_op jit(solution)/shard_map/project/pallas_call | solution.py:474
  136.2 2.3 %copy.9 = bf16[128,4096]{1,0:T(8,128)(2,1)} copy(bf16[128,4096]{1,0:T(8,128)(2,1)} %project.1) | data formatting | bytes 2097152

commit v2 on v1

--- a/solution.py
+++ b/solution.py
@@ -22,7 +22,11 @@
 NEG = -1e30
 C2 = D**-0.5 * math.log2(math.e)
 MESH = pl.DeviceIdType.MESH
-CHUNK = 8
+CHUNK = 16
+STEP = CHUNK * BLK
+FETCH = 8
+TALL = 2
+TALL_ROWS = TALL * ROWS
 
 
 def dot_t(a, b):
@@ -258,106 +262,154 @@
     )(vertical, slash, queries, keys, values)
 
 
-def vertical_kernel(vert, kv_ref, qx_ref, ov_ref, lv_ref, kc, vc, m_ref, l_ref, acc, sems):
+def vertical_kernel(
+    vert, kv_ref, qx_ref, ov_ref, lv_ref,
+    kc, vc, qt, m_ref, l_ref, acc, s0, s1, x0, x1, todo, sems, q_sem,
+):
     s = lax.axis_index("seq")
     x, p = s // 16, s % 16
-    step = CHUNK * BLK
-
-    def fetch(r):
+    q_copies = []
+    for i in range(RING):
+        for g in range(G):
+            c = pltpu.make_async_copy(
+                qx_ref.at[i, :, g * D : (g + 1) * D],
+                qt.at[pl.ds((i * G + g) * ROWS, ROWS)],
+                q_sem.at[i * G + g],
+            )
+            c.start()
+            q_copies.append(c)
+
+    def begin(r, unused):
         b = vert[x, r]
         slab = b // NB
         before = vert[x, jnp.maximum(r - 1, 0)] // NB
         slot = jnp.where((r > 0) & (before == slab), 1, 0)
         rows = pl.ds(pl.multiple_of(r * BLK, BLK), BLK)
         src = kv_ref.at[slab % 16, slab // 16]
-        return (
-            pltpu.make_async_copy(src.at[slot], kc.at[rows], sems.at[0, r // CHUNK]),
-            pltpu.make_async_copy(src.at[2 + slot], vc.at[rows], sems.at[1, r // CHUNK]),
-        )
-
-    def begin(r, unused):
-        for c in fetch(r):
-            c.start()
+        pltpu.make_async_copy(src.at[slot], kc.at[rows], sems.at[0, r // FETCH]).start()
+        pltpu.make_async_copy(src.at[2 + slot], vc.at[rows], sems.at[1, r // FETCH]).start()
         return unused
 
     lax.fori_loop(0, NV, begin, 0)
-
-    def count(i):
+    m_ref[...] = jnp.full(m_ref.shape, NEG, jnp.float32)
+    l_ref[...] = jnp.zeros(l_ref.shape, jnp.float32)
+    acc[...] = jnp.zeros(acc.shape, jnp.float32)
+
+    steps = jnp.int32(0)
+    for i in range(RING):
         limit = (i * 16 + p - 1) * NB
-        return lax.fori_loop(
-            0, NV, lambda r, n: n + jnp.where(vert[x, r] < limit, 1, 0), jnp.int32(0), unroll=8
-        )
-
-    for c in range(NV // CHUNK):
-        rows = pl.ds(c * step, step)
+        n = lax.fori_loop(
+            0, NV, lambda r, n: n + jnp.where(vert[x, r] < limit, 1, 0), jnp.int32(0), unroll=16
+        )
+
+        def put(c, t):
+            for u in range(G // TALL):
+                todo[t + u, 0] = (i * G + u * TALL) * ROWS
+                todo[t + u, 1] = c * STEP
+                todo[t + u, 2] = n * BLK - c * STEP
+            return t + G // TALL
+
+        steps = lax.fori_loop(0, (n + CHUNK - 1) // CHUNK, put, steps)
+    for e in range(2):
+        todo[steps + e, 0] = RING * G * ROWS
+        todo[steps + e, 1] = 0
+        todo[steps + e, 2] = STEP
+
+    for c in q_copies:
+        c.wait()
+    for c in range(NV // FETCH):
+        rows = pl.ds(c * FETCH * BLK, FETCH * BLK)
         pltpu.make_async_copy(kc.at[rows], kc.at[rows], sems.at[0, c]).wait()
         pltpu.make_async_copy(vc.at[rows], vc.at[rows], sems.at[1, c]).wait()
 
-    def slab_step(i, unused):
-        n = count(i)
-        full = n // CHUNK
-        m_ref[...] = jnp.full(m_ref.shape, NEG, jnp.float32)
-        l_ref[...] = jnp.zeros(l_ref.shape, jnp.float32)
-        acc[...] = jnp.zeros(acc.shape, jnp.float32)
-
-        def chunk(c, masked):
-            rows = pl.ds(pl.multiple_of(c * step, step), step)
-            ks, vs = kc[rows, :], vc[rows, :]
-            for g in range(G):
-                q = qx_ref[i, :, g * D : (g + 1) * D]
-                scores = dot_t(q, ks)
-                if masked:
-                    u = lax.broadcasted_iota(jnp.int32, (1, step), 1) + c * step
-                    scores = jnp.where(u < n * BLK, scores, NEG)
-                old = m_ref[g]
-                top = jnp.maximum(old, jnp.max(scores, axis=1, keepdims=True))
-                shrink = jnp.exp2((old - top) * C2)
-                weights = jnp.exp2((scores - top[:, :1]) * C2)
-                l_ref[g] = l_ref[g] * shrink + jnp.sum(weights, axis=1, keepdims=True)
-                acc[g] = acc[g] * shrink + dot_n(weights.astype(jnp.bfloat16), vs)
-                m_ref[g] = top
-
-        lax.fori_loop(0, full, lambda c, u: (chunk(c, False), u)[1], 0)
-
-        @pl.when(full * CHUNK < n)
-        def _():
-            chunk(full, True)
-
-        lane = lax.broadcasted_iota(jnp.int32, (ROWS, D), 1)
+    lanes = lax.broadcasted_iota(jnp.int32, (1, STEP), 1)
+
+    def score(t, s_ref, x_ref):
+        row, key = pl.multiple_of(todo[t, 0], ROWS), pl.multiple_of(todo[t, 1], STEP)
+        scores = dot_t(qt[pl.ds(row, TALL_ROWS), :], kc[pl.ds(key, STEP), :])
+        scores = jnp.where(lanes < todo[t, 2], scores, NEG)
+        s_ref[...] = scores
+        top = scores[:, :D]
+        for k in range(1, STEP // D):
+            top = jnp.maximum(top, scores[:, k * D : (k + 1) * D])
+        x_ref[...] = jnp.broadcast_to(jnp.max(top, axis=1, keepdims=True), (TALL_ROWS, D))
+
+    def weigh(t, s_ref, x_ref):
+        row, key = pl.multiple_of(todo[t, 0], ROWS), pl.multiple_of(todo[t, 1], STEP)
+        r = pl.ds(row, TALL_ROWS)
+        old = m_ref[r, :]
+        top = jnp.maximum(old, x_ref[...])
+        shrink = jnp.exp2((old - top) * C2)
+        rounded, sums = [], None
+        for k in range(STEP // D):
+            w = jnp.exp2((s_ref[:, k * D : (k + 1) * D] - top) * C2)
+            sums = w if sums is None else sums + w
+            rounded.append(w.astype(jnp.bfloat16))
+        l_ref[r, :] = l_ref[r, :] * shrink + sums
+        acc[r, :] = acc[r, :] * shrink + dot_n(
+            jnp.concatenate(rounded, axis=1), vc[pl.ds(key, STEP), :]
+        )
+        m_ref[r, :] = top
+
+    @pl.when(steps > 0)
+    def _():
+        score(0, s0, x0)
+
+        def pair(h, unused):
+            t = 2 * h
+            score(t + 1, s1, x1)
+            weigh(t, s0, x0)
+            score(t + 2, s0, x0)
+            weigh(t + 1, s1, x1)
+            return unused
+
+        lax.fori_loop(0, (steps + 1) // 2, pair, 0)
+
+    lane = lax.broadcasted_iota(jnp.int32, (ROWS, D), 1)
+
+    def finish(i, unused):
         levels = jnp.full((ROWS, D), NEG, jnp.float32)
         for g in range(G):
-            total = l_ref[g]
+            r = pl.ds(pl.multiple_of((i * G + g) * ROWS, ROWS), ROWS)
+            total = jnp.sum(l_ref[r, :], axis=1, keepdims=True)
             some = total > 0.0
             safe = jnp.where(some, total, 1.0)
-            ov_ref[i, :, g * D : (g + 1) * D] = (acc[g] / safe).astype(jnp.bfloat16)
-            level = jnp.where(some, m_ref[g] * C2 + jnp.log2(safe), NEG)
+            ov_ref[i, :, g * D : (g + 1) * D] = (acc[r, :] * (1.0 / safe)).astype(jnp.bfloat16)
+            level = jnp.where(some, m_ref[r, :] * C2 + jnp.log2(safe), NEG)
             levels = jnp.where(lane == g, level, levels)
         lv_ref[i] = levels.T[:8, :]
         return unused
 
-    lax.fori_loop(0, RING, slab_step, 0)
+    lax.fori_loop(0, RING, finish, 0)
 
 
 def vertical_part(vertical, kv, qx):
     bf16, f32 = jnp.bfloat16, jnp.float32
     vmem = pl.BlockSpec(memory_space=pltpu.VMEM)
+    hbm = pl.BlockSpec(memory_space=pl.ANY)
+    rows = RING * G * ROWS + TALL_ROWS
     return pl.pallas_call(
         vertical_kernel,
         out_shape=(
             jax.ShapeDtypeStruct((RING, ROWS, G * D), bf16),
             jax.ShapeDtypeStruct((RING, 8, ROWS), f32),
         ),
-        in_specs=[
-            pl.BlockSpec(memory_space=pltpu.SMEM), pl.BlockSpec(memory_space=pl.ANY), vmem,
-        ],
+        in_specs=[pl.BlockSpec(memory_space=pltpu.SMEM), hbm, hbm],
         out_specs=(vmem, vmem),
         scratch_shapes=[
             pltpu.VMEM((NV * BLK, D), bf16),
             pltpu.VMEM((NV * BLK, D), bf16),
-            pltpu.VMEM((G, ROWS, D), f32),
-            pltpu.VMEM((G, ROWS, D), f32),
-            pltpu.VMEM((G, ROWS, D), f32),
-            pltpu.SemaphoreType.DMA((2, NV // CHUNK)),
+            pltpu.VMEM((rows, D), bf16),
+            pltpu.VMEM((rows, D), f32),
+            pltpu.VMEM((rows, D), f32),
+            pltpu.VMEM((rows, D), f32),
+            pltpu.VMEM((TALL_ROWS, STEP), f32),
+            pltpu.VMEM((TALL_ROWS, STEP), f32),
+            pltpu.VMEM((TALL_ROWS, D), f32),
+            pltpu.VMEM((TALL_ROWS, D), f32),
+            pltpu.SMEM((RING * (G // TALL) * (NV // CHUNK) + 4, 3), jnp.int32),
+            pltpu.SemaphoreType.DMA((2, NV // FETCH)),
+            pltpu.SemaphoreType.DMA((RING * G,)),
         ],
         name="verticals",
     )(vertical, kv, qx)

time: 139 us -> 113 us (0.81)
  the two profiles are of different devices: /device:TPU:121 before, /device:TPU:25 now
where the time goes in v2:
time: 113 us
  Pallas kernels  109 us (96%)
  local copies, waits for them, and re-layouts  3.62 us (3%)
    pallas_call x1, Pallas kernels, exchange(): pl.pallas_call(exchange_kernel, out_shape=(jax.ShapeDtypeStruct((PLANE, R...  54.2 us
    pallas_call x1, Pallas kernels, project(): pl.pallas_call(project_kernel, out_shape=jax.ShapeDtypeStruct((ROWS // 2,...  28 us
    pallas_call x1, Pallas kernels, vertical_part(): pl.pallas_call(vertical_kernel, out_shape=(jax.ShapeDtypeStruct((RING, RO...  26.7 us
    unnamed x2, local copies, waits for them, and re-layouts  3.62 us

profile of v2, /device:TPU:25, one launch (start us, length us, event | category | flops | bytes accessed | tf_op | source)
XLA Modules:
  0.0 112.5 jit_solution(9544780608453082298)
XLA Ops:
  0.0 1.3 %copy.7.slash = s32[4,2]{1,0:T(4,128)} copy(s32[4,2]{0,1:T(2,128)} %param.10) | data formatting | bytes 64 | tf_op args[4]
  1.3 54.2 %exchange.1 = (bf16[16,4,4,64,128]{4,3,2,1,0:T(8,128)(2,1)}, bf16[4,256,512]{2,1,0:T(8,128)(2,1)}, f32[256,2048]{1,0:T(8,128)}, f32[256,128]{1,0:T(8,128)}) custom-call(s32[4,64]{1,0:T(4,128)} %vert.3, s32[4,2]{1,0:T(4,128)} %copy.7.slash, bf16[256,2048]{1,0:T(8,128)(2,1)} %q_ref.1, bf16[256,512]{1,0:T(8,128)(2,1)} %k_ref.1, bf16[256,512]{1,0:T(8,128)(2,1)} %v_ref.1), custom_call_target="tpu_custom_call" | custom-call | tf_op jit(solution)/shard_map/exchange/pallas_call | solution.py:241
  55.5 26.7 %verticals.1 = (bf16[4,256,512]{2,1,0:T(8,128)(2,1)}, f32[4,8,256]{2,1,0:T(8,128)}) custom-call(s32[4,64]{1,0:T(4,128)} %vert.3, bf16[16,4,4,64,128]{4,3,2,1,0:T(8,128)(2,1)} %get-tuple-element.11.kv_ref, bf16[4,256,512]{2,1,0:T(8,128)(2,1)} %get-tuple-element.12.qx_ref), custom_call_target="tpu_custom_call" | custom-call | tf_op jit(solution)/shard_map/verticals/pallas_call | solution.py:391
  82.2 28.0 %project.1 = bf16[128,4096]{1,0:T(8,128)(2,1)} custom-call(bf16[4,256,512]{2,1,0:T(8,128)(2,1)} %get-tuple-element.13.ov_ref, f32[4,8,256]{2,1,0:T(8,128)} %get-tuple-element.14.lv_ref, f32[256,2048]{1,0:T(8,128)} %get-tuple-element.15.ol_ref, f32[256,128]{1,0:T(8,128)} %get-tuple-element.16.ll_ref, bf16[2048,4096]{1,0:T(8,128)(2,1)} %w_hbm.1), custom_call_target="tpu_custom_call" | custom-call | tf_op jit(solution)/shard_map/project/pallas_call | solution.py:526
  110.2 2.3 %copy.9 = bf16[128,4096]{1,0:T(8,128)(2,1)} copy(bf16[128,4096]{1,0:T(8,128)(2,1)} %project.1) | data formatting | bytes 2097152
